TPU v7x, 32 devices: a whole 2x2x4 slice. The times are simulated.
32 devices in a mesh: order: 8 (over y, x, core), axial: 4 (over z).
Axes of the slice: x: 2, y: 2, z: 4, core: 2. Of those that a mesh axis runs over, the one named last changes fastest.
Arguments:
- coefficients: bfloat16 [4, 2, 1024, 8, 1024], P(None, None, 'order', 'axial'), may hold values from -0.005859375 to 0.005859375
- order_lists: int32 [1024], replicated, may hold values from 0 to 1023, as said below
- lengths: int32 [1024], replicated, may hold values from 128 to 1024, as said below
Outputs:
- advection: bfloat16 [3, 2, 1024, 8, 1024], P(None, None, 'order', 'axial')
Inputs may be any that keep to these rules, and one draw needn't show every extreme that they name: `order_lists`: a permutation of the orders 0 to 1023; the device with index j along order holds slots j * 128 to (j + 1) * 128 - 1 of coefficients and advection. lengths[m] minus (128 + ((1023 - m) * 768) // 1023) lies in 0 to 128.
All inputs are finite; a program needn't handle non-finite values.
Results may differ from a plain program's by a relative error of at most 0.0095.
Values may be sent and summed in bfloat16 or wider, within the bound.
A program may use at most 128 MiB of HBM per device.

v0:
```python
import math
import jax
import jax.numpy as jnp
from jax import lax
from jax.sharding import PartitionSpec as P

R = 1024


def with_halo(block, sides, width):
    for axis, dim in sides:
        count = lax.axis_size(axis)
        forward = [(i, i + 1) for i in range(count - 1)]
        forward.append((count - 1, 0))
        backward = [(target, source) for source, target in forward]
        low = lax.ppermute(
            lax.slice_in_dim(block, block.shape[dim] - width, None, axis=dim), axis, forward
        )
        high = lax.ppermute(lax.slice_in_dim(block, 0, width, axis=dim), axis, backward)
        block = jnp.concatenate([low, block, high], axis=dim)
    return block


def radial_tables(radius_count, mode_count):
    radius_ids = jnp.arange(radius_count, dtype=jnp.int32)
    mode_ids = jnp.arange(mode_count, dtype=jnp.int32)
    phases = mode_ids[None, :] * (2 * radius_ids[:, None] + 1) % (4 * radius_count)
    angles_rad = phases.astype(jnp.float32) * (math.pi / (2 * radius_count))
    synthesis = jnp.cos(angles_rad).astype(jnp.bfloat16)
    analysis = (jnp.cos(angles_rad.T) * math.sqrt(2.0 / radius_count)).astype(jnp.bfloat16)
    return (synthesis, analysis)


def azimuthal_tables(order_ids, point_count):
    points = jnp.arange(point_count, dtype=jnp.int32)
    phases = order_ids[..., None] * points % point_count
    angles_rad = phases.astype(jnp.float32) * (2.0 * math.pi / point_count)
    cosines = jnp.cos(angles_rad)
    sines = jnp.sin(angles_rad)
    weight = jnp.where(order_ids == 0, 1.0, 2.0).astype(jnp.float32)[..., None]
    forward = jnp.stack((weight * cosines, -weight * sines), axis=-3).astype(jnp.bfloat16)
    factor = math.sqrt(2.0 / point_count)
    inverse = jnp.stack((cosines * factor, -sines * factor), axis=-3).astype(jnp.bfloat16)
    return (forward, inverse)


def shards(coefficients, order_lists, lengths):
    field_count, part_count, slot_count, plane_count, mode_count = coefficients.shape
    order_count = order_lists.shape[0]
    point_count = 2 * order_count
    radius_count = R
    group_count = lax.axis_size("order")
    band_width = radius_count // group_count
    synthesis, analysis = radial_tables(radius_count, mode_count)
    owned_ids = lax.dynamic_slice_in_dim(
        order_lists, lax.axis_index("order") * slot_count, slot_count
    )
    catalog = jnp.arange(order_count, dtype=jnp.int32)
    own_lengths = jnp.sum(
        jnp.where(owned_ids[:, None] == catalog[None, :], lengths[None, :], 0), axis=1
    )
    retained = jnp.arange(mode_count, dtype=jnp.int32)[None, :] < own_lengths[:, None]
    masked = jnp.where(
        retained[None, None, :, None, :], coefficients, jnp.zeros((), coefficients.dtype)
    )
    radial = jnp.einsum("fcmzk,rk->frzcm", masked, synthesis, preferred_element_type=jnp.float32)
    radial = radial.astype(jnp.bfloat16).reshape(
        field_count, radius_count, plane_count * part_count * slot_count
    )
    forward, inverse = azimuthal_tables(order_lists.reshape(group_count, slot_count), point_count)
    received = lax.all_to_all(radial, "order", split_axis=1, concat_axis=2, tiled=True)
    item_count = received.shape[0]
    lattice = received.reshape(
        item_count, band_width, group_count, plane_count, part_count, slot_count
    )
    physical = jnp.einsum(
        "frizcm,icmj->fzrj", lattice, forward, preferred_element_type=jnp.float32
    ).astype(jnp.bfloat16)
    padded = with_halo(physical[:3], (("axial", 1),), 2)
    widened = padded.astype(jnp.float32)
    gradient = (
        8.0 * (widened[:, 3 : plane_count + 3] - widened[:, 1 : plane_count + 1])
        - (widened[:, 4 : plane_count + 4] - widened[:, 0:plane_count])
    ) / 12.0
    products = (physical[3].astype(jnp.float32)[None] * gradient).astype(jnp.bfloat16)
    spectral = jnp.einsum(
        "gzrj,icmj->grizcm", products, inverse, preferred_element_type=jnp.float32
    )
    spectral = spectral.astype(jnp.bfloat16).reshape(
        3, band_width, group_count * plane_count * part_count * slot_count
    )
    received = lax.all_to_all(spectral, "order", split_axis=2, concat_axis=1, tiled=True)
    item_count = received.shape[0]
    lattice = received.reshape(item_count, radius_count, plane_count, part_count, slot_count)
    result = jnp.einsum("grzcm,kr->gcmzk", lattice, analysis, preferred_element_type=jnp.float32)
    return jnp.where(retained[None, None, :, None, :], result, 0.0).astype(jnp.bfloat16)


def solution(mesh):
    placed = (P(None, None, "order", "axial", None), P(), P())
    return jax.shard_map(
        shards,
        mesh=mesh,
        in_specs=placed,
        out_specs=P(None, None, "order", "axial", None),
        check_vma=False,
    )
```

profile of v0, /device:TPU:0, one launch (start us, length us, event | category | flops | bytes accessed | tf_op | source)
XLA Modules:
  0.0 382.5 jit_solution(8791086650537149125)
XLA Ops:
  0.0 0.8 dynamic_slice.3
  0.8 0.9 select_reduce_fusion
  1.6 0.1 iota_compare_fusion.1
  1.8 0.2 copy.46
  2.0 9.3 %broadcast_select_fusion = bf16[4,2,128,2,1024]{4,3,2,1,0:T(2,128)(2,1)} fusion(bf16[4,2,128,2,1024]{4,3,2,1,0:T(2,128)(2,1)} %param.3, pred[128,1024]{1,0:T(8,128)(4,1)S(1)} %copy.46), kind=kLoop, calls=%fused_computation.22 | loop fusion | flops 2097152 | bytes 8519680 | tf_op jit(solution)/shard_map/jit(_where)/select_n | solution.py:63
  11.3 21.9 %convert_bitcast_fusion = bf16[4,1024,2,2,128]{1,4,2,3,0:T(8,128)(2,1)S(1)} fusion(bf16[4,2,128,2,1024]{4,3,2,1,0:T(2,128)(2,1)} %broadcast_select_fusion, s32[1024]{0:T(1024)S(1)} %multiply_add_fusion), kind=kOutput, calls=%fused_computation.51 | convolution fusion | flops 4312793088 | bytes 8392704 | tf_op jit(solution)/shard_map/fcmzk,rk->frzcm/dot_general | solution.py:66
  33.3 2.4 copy.48
  35.7 7.8 %copy.49 = bf16[4,1024,512]{2,0,1:T(4,128)(2,1)} copy(bf16[4,1024,512]{1,2,0:T(8,128)(2,1)} %bitcast.66) | data formatting | bytes 8388608 | tf_op jit(solution)/shard_map/reshape | solution.py:67
  43.5 0.0 copy-start.2
  43.5 5.6 %all-to-all-start = ((bf16[4,1024,512]{2,0,1:T(4,128)(2,1)}), bf16[4,1024,512]{2,0,1:T(4,128)(2,1)}, u32[]{:S(2)}, u32[]{:S(2)}) async-start(bf16[4,1024,512]{2,0,1:T(4,128)(2,1)} %copy.49), calls=%async_computation | async-start | bytes 8388608 | tf_op jit(solution)/shard_map/all_to_all | solution.py:71
  49.1 0.0 copy-done.2
  49.2 38.0 %multiply_convert_fusion.3 = (bf16[8,1,128,2048]{2,3,0,1:T(8,128)(2,1)}, bf16[8,1,128,2048]{2,3,0,1:T(8,128)(2,1)}, bf16[8,1,128,2048]{2,3,0,1:T(8,128)(2,1)}, bf16[8,1,128,2048]{2,3,0,1:T(8,128)(2,1)}) fusion(s32[8,128]{1,0:T(8,128)S(1)} %bitcast.71, f32[8,128]{1,0:T(8,128)S(1)} %get-tuple-element.9, f32[8,128]{1,0:T(8,128)S(1)} %get-tuple-element.10), kind=kLoop, calls=%fused_computation.18 | loop fusion | flops 48234496 | bytes 16789504 | tf_op jit(solution)/shard_map/convert.2
  87.2 11.1 %all-to-all-done = bf16[4,1024,512]{2,0,1:T(4,128)(2,1)} async-done(((bf16[4,1024,512]{2,0,1:T(4,128)(2,1)}), bf16[4,1024,512]{2,0,1:T(4,128)(2,1)}, u32[]{:S(2)}, u32[]{:S(2)}) %all-to-all-start) | async-done | bytes 4194336 | tf_op jit(solution)/shard_map/all_to_all | solution.py:71
  98.3 3.0 copy.50
  101.3 0.0 copy-start
  101.3 0.0 copy-start.1
  101.3 2.4 copy.51
  103.8 0.0 copy-done
  103.8 1.0 copy-done.1
  104.8 9.2 %fusion.38 = bf16[4,2,128,2048]{2,3,1,0:T(8,128)(2,1)S(1)} fusion(bf16[4,128,8,2,2,128]{5,2,4,3,1,0:T(8,128)(2,1)S(1)} %bitcast.70, bf16[8,1,128,2048]{2,3,0,1:T(8,128)(2,1)S(1)} %copy-done.1, bf16[8,1,128,2048]{2,3,0,1:T(8,128)(2,1)S(1)} %copy-done), kind=kOutput, calls=%fused_computation.60 | convolution fusion | flops 8608808960 | bytes 16777216 | tf_op jit(solution)/shard_map/frizcm,icmj->fzrj/dot_general | solution.py:76
  114.0 0.2 slice.24
  114.2 4.4 %collective-permute-start.1 = (bf16[3,2,128,2048]{2,3,1,0:T(8,128)(2,1)S(1)}, bf16[3,2,128,2048]{2,3,1,0:T(8,128)(2,1)S(1)}, u32[]{:S(2)}, u32[]{:S(2)}) collective-permute-start(bf16[3,2,128,2048]{2,3,1,0:T(8,128)(2,1)S(1)} %slice.24), channel_id=1, source_target_pairs={{1,0},{2,1},{3,2},{0,3},{5,4},{6,5},{7,6},{4,7},{9,8},{10,9},{11,1... | collective-permute-start | bytes 9437192 | tf_op jit(solution)/shard_map/ppermute | solution.py:19
  118.6 0.0 collective-permute-start
  118.6 1.5 multiply_bitcast_fusion
  120.1 67.0 %collective-permute-done.1 = bf16[3,2,128,2048]{2,3,1,0:T(8,128)(2,1)S(1)} collective-permute-done((bf16[3,2,128,2048]{2,3,1,0:T(8,128)(2,1)S(1)}, bf16[3,2,128,2048]{2,3,1,0:T(8,128)(2,1)S(1)}, u32[]{:S(2)}, u32[]{:S(2)}) %collective-permute-start.1) | collective-permute-done | bytes 3145760 | tf_op jit(solution)/shard_map/ppermute | solution.py:19
  187.1 64.2 %collective-permute-done = bf16[3,2,128,2048]{2,3,1,0:T(8,128)(2,1)S(1)} collective-permute-done((bf16[3,2,128,2048]{2,3,1,0:T(8,128)(2,1)S(1)}, bf16[3,2,128,2048]{2,3,1,0:T(8,128)(2,1)S(1)}, u32[]{:S(2)}, u32[]{:S(2)}) %collective-permute-start) | collective-permute-done | bytes 3145760 | tf_op jit(solution)/shard_map/ppermute | solution.py:16
  251.3 7.1 %maximum_convert_fusion = f32[3,6,128,2048]{2,3,1,0:T(8,128)} fusion(bf16[3,2,128,2048]{2,3,1,0:T(8,128)(2,1)S(1)} %collective-permute-done.1, bf16[3,2,128,2048]{2,3,1,0:T(8,128)(2,1)S(1)} %slice.24, bf16[3,2,128,2048]{2,3,1,0:T(8,128)(2,1)S(1)} %collective-permute-done), kind=kLoop, calls=%fused_computation.3 | loop fusion | flops 14155776 | bytes 28311552 | tf_op jit(solution)/shard_map/convert_element_type | solution.py:80
  258.4 18.2 %convert_bitcast_fusion.1 = bf16[3,128,8,2,2,128]{1,5,3,0,4,2:T(8,128)(2,1)S(1)} fusion(f32[2,128,2048]{1,2,0:T(8,128)} %multiply_bitcast_fusion, f32[3,6,128,2048]{2,3,1,0:T(8,128)} %maximum_convert_fusion, bf16[8,1,128,2048]{2,3,0,1:T(8,128)(2,1)} %get-tuple-element.7, bf16[8,1,128,2048]{2,3,0,1:T(8,128)(2,1)} %get-tuple-element.5), kind=kOutput, calls=%fused_computation.63 | convolution fusion | flops 6457655296 | bytes 38797312 | tf_op jit(solution)/shard_map/gzrj,icmj->grizcm/dot_general | solution.py:86
  276.6 0.2 copy.55
  276.8 20.0 %copy.56 = bf16[3,128,4096]{1,0,2:T(4,128)(2,1)S(1)} copy(bf16[3,128,4096]{1,2,0:T(8,128)(2,1)S(1)} %bitcast.68) | data formatting | bytes 6291456 | tf_op jit(solution)/shard_map/reshape | solution.py:89
  296.8 53.8 %all_to_all.30 = bf16[3,128,4096]{1,0,2:T(4,128)(2,1)S(1)} all-to-all(bf16[3,128,4096]{1,0,2:T(4,128)(2,1)S(1)} %copy.56), channel_id=1, replica_groups=mesh['order'=8,'axial'=4] {'order'}, dimensions={2} | all-to-all | bytes 6291456 | tf_op jit(solution)/shard_map/all_to_all | solution.py:92
  350.6 2.6 copy.83
  353.2 3.3 reshape.125
  356.5 20.2 %fusion.15 = bf16[3,2,128,2,1024]{2,4,1,3,0:T(8,128)(2,1)S(1)} fusion(pred[128,1024]{0,1:T(8,128)(4,1)S(1)} %iota_compare_fusion.1, bf16[3,1024,2,2,128]{1,4,3,2,0:T(8,128)(2,1)} %reshape.125, s32[1024]{0:T(1024)S(1)} %multiply_add_fusion), kind=kOutput, calls=%fused_computation.30 | convolution fusion | flops 3241148416 | bytes 6426624 | tf_op jit(solution)/shard_map/grzcm,kr->gcmzk/dot_general | solution.py:95
  376.7 5.6 %copy.59 = bf16[3,2,128,2,1024]{4,3,2,1,0:T(2,128)(2,1)} copy(bf16[3,2,128,2,1024]{2,4,1,3,0:T(8,128)(2,1)S(1)} %fusion.15) | data formatting | bytes 6291456 | tf_op jit(solution)/shard_map/convert_element_type | solution.py:96
  (2 shorter events, 0.0 us)
Async XLA Ops:
  43.5 5.6 %copy-start.2 = (s32[1024]{0:T(1024)S(1)}, s32[1024]{0:T(1024)}, u32[]{:S(2)}) copy-start(s32[1024]{0:T(1024)} %param.4) | copy-start | bytes 12292
  43.5 54.8 %all-to-all-start = ((bf16[4,1024,512]{2,0,1:T(4,128)(2,1)}), bf16[4,1024,512]{2,0,1:T(4,128)(2,1)}, u32[]{:S(2)}, u32[]{:S(2)}) async-start(bf16[4,1024,512]{2,0,1:T(4,128)(2,1)} %copy.49), calls=%async_computation | async-start | bytes 8388608 | tf_op jit(solution)/shard_map/all_to_all | solution.py:71
  101.3 2.4 copy-start
  101.3 3.5 copy-start.1
  114.2 72.9 %collective-permute-start.1 = (bf16[3,2,128,2048]{2,3,1,0:T(8,128)(2,1)S(1)}, bf16[3,2,128,2048]{2,3,1,0:T(8,128)(2,1)S(1)}, u32[]{:S(2)}, u32[]{:S(2)}) collective-permute-start(bf16[3,2,128,2048]{2,3,1,0:T(8,128)(2,1)S(1)} %slice.24), channel_id=1, source_target_pairs={{1,0},{2,1},{3,2},{0,3},{5,4},{6,5},{7,6},{4,7},{9,8},{10,9},{11,1... | collective-permute-start | bytes 9437192 | tf_op jit(solution)/shard_map/ppermute | solution.py:19
  118.6 132.7 %collective-permute-start = (bf16[3,2,128,2048]{2,3,1,0:T(8,128)(2,1)S(1)}, bf16[3,2,128,2048]{2,3,1,0:T(8,128)(2,1)S(1)}, u32[]{:S(2)}, u32[]{:S(2)}) collective-permute-start(bf16[3,2,128,2048]{2,3,1,0:T(8,128)(2,1)S(1)} %slice.24), channel_id=1, source_target_pairs={{0,1},{1,2},{2,3},{3,0},{4,5},{5,6},{6,7},{7,4},{8,9},{9,10},{10,1... | collective-permute-start | bytes 9437192 | tf_op jit(solution)/shard_map/ppermute | solution.py:16
where the time goes:
time: 388 us; the launch traced here: 382 us
  waiting for transfers between devices  142 us (37%)
  matrix products  69.5 us (18%)
  other arithmetic  56.9 us (15%)
  blocking collectives  53.8 us (14%)
  local copies, waits for them, and re-layouts  49.6 us (13%)
  starting transfers between devices  9.99 us (3%)
    ppermute x1, waiting for transfers between devices, with_halo(): lax.ppermute(lax.slice_in_dim(block, 0, width, axis=dim), axis, backward)  67 us
    ppermute x1, waiting for transfers between devices, with_halo(): lax.ppermute(lax.slice_in_dim(block, block.shape[dim] - width, None, axis...  64.2 us
    all_to_all x1, blocking collectives, shards(): lax.all_to_all(spectral, 'order', split_axis=2, concat_axis=1, tiled=True)  53.8 us
    another operation x1, other arithmetic  38 us
    dot_general x1, matrix products, shards(): jnp.einsum('fcmzk,rk->frzcm', masked, synthesis, preferred_element_type=j...  21.9 us
    dot_general x1, matrix products, shards(): jnp.einsum('grzcm,kr->gcmzk', lattice, analysis, preferred_element_type=j...  20.2 us
    reshape x1, local copies, waits for them, and re-layouts, shards(): spectral.astype(jnp.bfloat16)  20 us
    dot_general x1, matrix products, shards(): jnp.einsum('gzrj,icmj->grizcm', products, inverse, preferred_element_type...  18.2 us
  transfers between devices with their start and end apart: 3, of which 3 were waited for; matrix products, arithmetic and copies ran while one was open for 10% of the time, Pallas kernels for 0%

commit v1 on v0

--- a/solution.py
+++ b/solution.py
@@ -89,7 +89,12 @@
     spectral = spectral.astype(jnp.bfloat16).reshape(
         3, band_width, group_count * plane_count * part_count * slot_count
     )
-    received = lax.all_to_all(spectral, "order", split_axis=2, concat_axis=1, tiled=True)
+    received = jnp.concatenate(
+        lax.all_to_all(
+            jnp.stack(jnp.split(spectral, lax.axis_size("order"), axis=2)), "order", 0, 0
+        ),
+        axis=1,
+    )
     item_count = received.shape[0]
     lattice = received.reshape(item_count, radius_count, plane_count, part_count, slot_count)
     result = jnp.einsum("grzcm,kr->gcmzk", lattice, analysis, preferred_element_type=jnp.float32)

time: 388 us -> 357 us (0.920)
  local copies, waits for them, and re-layouts: 49.6 us -> 29.5 us
  blocking collectives: 53.8 us -> 42.8 us
    reshape x2 -> x1, local copies, waits for them, and re-layouts: 23.3 us -> 2.03 us  [shards(): jnp.concatenate(lax.all_to_all(jnp.stack(jnp.split(spectral, lax.axis_siz...]
    all_to_all x1, blocking collectives: 53.8 us -> 42.8 us  [shards(): lax.all_to_all(jnp.stack(jnp.split(spectral, lax.axis_size('order'), axis...]
  transfers between devices with their start and end apart: 3 -> 3, of which waited for: 3 -> 3; matrix products, arithmetic and copies ran while one was open for 10% -> 11% of each run, Pallas kernels for 0% -> 0%
where the time goes in v1:
time: 357 us; the launch traced here: 351 us
  waiting for transfers between devices  142 us (40%)
  matrix products  69.7 us (20%)
  other arithmetic  56.7 us (16%)
  blocking collectives  42.8 us (12%)
  local copies, waits for them, and re-layouts  29.5 us (8%)
  starting transfers between devices  9.97 us (3%)
    ppermute x1, waiting for transfers between devices, with_halo(): lax.ppermute(lax.slice_in_dim(block, 0, width, axis=dim), axis, backward)  67 us
    ppermute x1, waiting for transfers between devices, with_halo(): lax.ppermute(lax.slice_in_dim(block, block.shape[dim] - width, None, axis...  64.2 us
    all_to_all x1, blocking collectives, shards(): lax.all_to_all(jnp.stack(jnp.split(spectral, lax.axis_size('order'), axis...  42.8 us
    another operation x1, other arithmetic  38 us
    dot_general x1, matrix products, shards(): jnp.einsum('fcmzk,rk->frzcm', masked, synthesis, preferred_element_type=j...  22.2 us
    dot_general x1, matrix products, shards(): jnp.einsum('grzcm,kr->gcmzk', lattice, analysis, preferred_element_type=j...  20 us
    dot_general x1, matrix products, shards(): jnp.einsum('gzrj,icmj->grizcm', products, inverse, preferred_element_type...  18.2 us
    all_to_all x1, waiting for transfers between devices, shards(): lax.all_to_all(radial, 'order', split_axis=1, concat_axis=2, tiled=True)  11.1 us
  transfers between devices with their start and end apart: 3, of which 3 were waited for; matrix products, arithmetic and copies ran while one was open for 11% of the time, Pallas kernels for 0%

profile of v1, /device:TPU:0, one launch (start us, length us, event | category | flops | bytes accessed | tf_op | source)
XLA Modules:
  0.0 351.4 jit_solution(5074464116270954435)
XLA Ops:
  0.0 0.8 dynamic_slice.3
  0.8 0.9 select_reduce_fusion
  1.6 0.1 iota_compare_fusion.1
  1.8 0.2 copy.44
  2.0 9.3 %broadcast_select_fusion = bf16[4,2,128,2,1024]{4,3,2,1,0:T(2,128)(2,1)} fusion(bf16[4,2,128,2,1024]{4,3,2,1,0:T(2,128)(2,1)} %param.3, pred[128,1024]{1,0:T(8,128)(4,1)S(1)} %copy.44), kind=kLoop, calls=%fused_computation.22 | loop fusion | flops 2097152 | bytes 8519680 | tf_op jit(solution)/shard_map/jit(_where)/select_n | solution.py:63
  11.3 22.2 %convert_bitcast_fusion = bf16[4,1024,2,2,128]{1,4,2,3,0:T(8,128)(2,1)S(1)} fusion(bf16[4,2,128,2,1024]{4,3,2,1,0:T(2,128)(2,1)} %broadcast_select_fusion, s32[1024]{0:T(1024)S(1)} %multiply_add_fusion), kind=kOutput, calls=%fused_computation.51 | convolution fusion | flops 4312793088 | bytes 8392704 | tf_op jit(solution)/shard_map/fcmzk,rk->frzcm/dot_general | solution.py:66
  33.6 2.4 copy.46
  36.0 7.8 %copy.47 = bf16[4,1024,512]{2,0,1:T(4,128)(2,1)} copy(bf16[4,1024,512]{1,2,0:T(8,128)(2,1)} %bitcast.94) | data formatting | bytes 8388608 | tf_op jit(solution)/shard_map/reshape | solution.py:67
  43.8 0.0 copy-start.2
  43.8 5.5 %all-to-all-start = ((bf16[4,1024,512]{2,0,1:T(4,128)(2,1)}), bf16[4,1024,512]{2,0,1:T(4,128)(2,1)}, u32[]{:S(2)}, u32[]{:S(2)}) async-start(bf16[4,1024,512]{2,0,1:T(4,128)(2,1)} %copy.47), calls=%async_computation | async-start | bytes 8388608 | tf_op jit(solution)/shard_map/all_to_all | solution.py:71
  49.4 0.0 copy-done.2
  49.4 38.0 %multiply_convert_fusion.3 = (bf16[8,1,128,2048]{2,3,0,1:T(8,128)(2,1)}, bf16[8,1,128,2048]{2,3,0,1:T(8,128)(2,1)}, bf16[8,1,128,2048]{2,3,0,1:T(8,128)(2,1)}, bf16[8,1,128,2048]{2,3,0,1:T(8,128)(2,1)}) fusion(s32[8,128]{1,0:T(8,128)S(1)} %bitcast.106, f32[8,128]{1,0:T(8,128)S(1)} %get-tuple-element.9, f32[8,128]{1,0:T(8,128)S(1)} %get-tuple-element.10), kind=kLoop, calls=%fused_computation.18 | loop fusion | flops 48234496 | bytes 16789504 | tf_op jit(solution)/shard_map/convert.2
  87.4 11.1 %all-to-all-done = bf16[4,1024,512]{2,0,1:T(4,128)(2,1)} async-done(((bf16[4,1024,512]{2,0,1:T(4,128)(2,1)}), bf16[4,1024,512]{2,0,1:T(4,128)(2,1)}, u32[]{:S(2)}, u32[]{:S(2)}) %all-to-all-start) | async-done | bytes 4194336 | tf_op jit(solution)/shard_map/all_to_all | solution.py:71
  98.5 3.0 copy.48
  101.6 0.0 copy-start
  101.6 0.0 copy-start.1
  101.6 2.4 copy.49
  104.0 0.0 copy-done
  104.0 1.0 copy-done.1
  105.0 9.2 %fusion.38 = bf16[4,2,128,2048]{2,3,1,0:T(8,128)(2,1)S(1)} fusion(bf16[4,128,8,2,2,128]{5,2,4,3,1,0:T(8,128)(2,1)S(1)} %bitcast.105, bf16[8,1,128,2048]{2,3,0,1:T(8,128)(2,1)S(1)} %copy-done.1, bf16[8,1,128,2048]{2,3,0,1:T(8,128)(2,1)S(1)} %copy-done), kind=kOutput, calls=%fused_computation.60 | convolution fusion | flops 8608808960 | bytes 16777216 | tf_op jit(solution)/shard_map/frizcm,icmj->fzrj/dot_general | solution.py:76
  114.3 0.2 slice.24
  114.5 4.4 %collective-permute-start.1 = (bf16[3,2,128,2048]{2,3,1,0:T(8,128)(2,1)S(1)}, bf16[3,2,128,2048]{2,3,1,0:T(8,128)(2,1)S(1)}, u32[]{:S(2)}, u32[]{:S(2)}) collective-permute-start(bf16[3,2,128,2048]{2,3,1,0:T(8,128)(2,1)S(1)} %slice.24), channel_id=1, source_target_pairs={{1,0},{2,1},{3,2},{0,3},{5,4},{6,5},{7,6},{4,7},{9,8},{10,9},{11,1... | collective-permute-start | bytes 9437192 | tf_op jit(solution)/shard_map/ppermute | solution.py:19
  118.9 0.0 collective-permute-start
  118.9 1.5 multiply_bitcast_fusion
  120.4 67.0 %collective-permute-done.1 = bf16[3,2,128,2048]{2,3,1,0:T(8,128)(2,1)S(1)} collective-permute-done((bf16[3,2,128,2048]{2,3,1,0:T(8,128)(2,1)S(1)}, bf16[3,2,128,2048]{2,3,1,0:T(8,128)(2,1)S(1)}, u32[]{:S(2)}, u32[]{:S(2)}) %collective-permute-start.1) | collective-permute-done | bytes 3145760 | tf_op jit(solution)/shard_map/ppermute | solution.py:19
  187.4 64.2 %collective-permute-done = bf16[3,2,128,2048]{2,3,1,0:T(8,128)(2,1)S(1)} collective-permute-done((bf16[3,2,128,2048]{2,3,1,0:T(8,128)(2,1)S(1)}, bf16[3,2,128,2048]{2,3,1,0:T(8,128)(2,1)S(1)}, u32[]{:S(2)}, u32[]{:S(2)}) %collective-permute-start) | collective-permute-done | bytes 3145760 | tf_op jit(solution)/shard_map/ppermute | solution.py:16
  251.6 6.9 %maximum_convert_fusion = f32[3,6,128,2048]{2,3,1,0:T(8,128)} fusion(bf16[3,2,128,2048]{2,3,1,0:T(8,128)(2,1)S(1)} %collective-permute-done.1, bf16[3,2,128,2048]{2,3,1,0:T(8,128)(2,1)S(1)} %slice.24, bf16[3,2,128,2048]{2,3,1,0:T(8,128)(2,1)S(1)} %collective-permute-done), kind=kLoop, calls=%fused_computation.3 | loop fusion | flops 14155776 | bytes 28311552 | tf_op jit(solution)/shard_map/convert_element_type | solution.py:80
  258.5 18.2 %convert_bitcast_fusion.1 = bf16[3,128,8,2,2,128]{1,5,3,0,4,2:T(8,128)(2,1)S(1)} fusion(f32[2,128,2048]{1,2,0:T(8,128)} %multiply_bitcast_fusion, f32[3,6,128,2048]{2,3,1,0:T(8,128)} %maximum_convert_fusion, bf16[8,1,128,2048]{2,3,0,1:T(8,128)(2,1)} %get-tuple-element.7, bf16[8,1,128,2048]{2,3,0,1:T(8,128)(2,1)} %get-tuple-element.5), kind=kOutput, calls=%fused_computation.62 | convolution fusion | flops 6457655296 | bytes 38797312 | tf_op jit(solution)/shard_map/gzrj,icmj->grizcm/dot_general | solution.py:86
  276.7 0.2 copy.53
  276.9 0.1 fusion.71
  277.0 0.1 fusion.70
  277.0 0.1 fusion.69
  277.1 0.1 fusion.68
  277.2 0.1 fusion.67
  277.2 0.1 fusion.66
  277.3 0.1 fusion.65
  277.4 42.8 %all_to_all.20 = bf16[8,3,128,512]{2,3,1,0:T(8,128)(2,1)S(1)} all-to-all(bf16[8,3,128,512]{2,3,1,0:T(8,128)(2,1)S(1)} %fusion.65), channel_id=1, replica_groups=mesh['order'=8,'axial'=4] {'order'}, dimensions={0} | all-to-all | bytes 6291456 | tf_op jit(solution)/shard_map/all_to_all | solution.py:93
  320.1 2.0 copy.54
  322.2 3.3 reshape_reshape.3
  325.5 20.0 %fusion.15 = bf16[3,2,128,2,1024]{2,4,1,3,0:T(8,128)(2,1)S(1)} fusion(pred[128,1024]{0,1:T(8,128)(4,1)S(1)} %iota_compare_fusion.1, bf16[3,1024,2,2,128]{1,4,3,2,0:T(8,128)(2,1)} %reshape_reshape.3, s32[1024]{0:T(1024)S(1)} %multiply_add_fusion), kind=kOutput, calls=%fused_computation.30 | convolution fusion | flops 3241148416 | bytes 6426624 | tf_op jit(solution)/shard_map/grzcm,kr->gcmzk/dot_general | solution.py:100
  345.5 5.6 %copy.56 = bf16[3,2,128,2,1024]{4,3,2,1,0:T(2,128)(2,1)} copy(bf16[3,2,128,2,1024]{2,4,1,3,0:T(8,128)(2,1)S(1)} %fusion.15) | data formatting | bytes 6291456 | tf_op jit(solution)/shard_map/convert_element_type | solution.py:101
  (3 shorter events, 0.0 us)
Async XLA Ops:
  43.8 5.6 %copy-start.2 = (s32[1024]{0:T(1024)S(1)}, s32[1024]{0:T(1024)}, u32[]{:S(2)}) copy-start(s32[1024]{0:T(1024)} %param.4) | copy-start | bytes 12292
  43.8 54.7 %all-to-all-start = ((bf16[4,1024,512]{2,0,1:T(4,128)(2,1)}), bf16[4,1024,512]{2,0,1:T(4,128)(2,1)}, u32[]{:S(2)}, u32[]{:S(2)}) async-start(bf16[4,1024,512]{2,0,1:T(4,128)(2,1)} %copy.47), calls=%async_computation | async-start | bytes 8388608 | tf_op jit(solution)/shard_map/all_to_all | solution.py:71
  101.6 2.4 copy-start
  101.6 3.5 copy-start.1
  114.5 72.9 %collective-permute-start.1 = (bf16[3,2,128,2048]{2,3,1,0:T(8,128)(2,1)S(1)}, bf16[3,2,128,2048]{2,3,1,0:T(8,128)(2,1)S(1)}, u32[]{:S(2)}, u32[]{:S(2)}) collective-permute-start(bf16[3,2,128,2048]{2,3,1,0:T(8,128)(2,1)S(1)} %slice.24), channel_id=1, source_target_pairs={{1,0},{2,1},{3,2},{0,3},{5,4},{6,5},{7,6},{4,7},{9,8},{10,9},{11,1... | collective-permute-start | bytes 9437192 | tf_op jit(solution)/shard_map/ppermute | solution.py:19
  118.9 132.7 %collective-permute-start = (bf16[3,2,128,2048]{2,3,1,0:T(8,128)(2,1)S(1)}, bf16[3,2,128,2048]{2,3,1,0:T(8,128)(2,1)S(1)}, u32[]{:S(2)}, u32[]{:S(2)}) collective-permute-start(bf16[3,2,128,2048]{2,3,1,0:T(8,128)(2,1)S(1)} %slice.24), channel_id=1, source_target_pairs={{0,1},{1,2},{2,3},{3,0},{4,5},{5,6},{6,7},{7,4},{8,9},{9,10},{10,1... | collective-permute-start | bytes 9437192 | tf_op jit(solution)/shard_map/ppermute | solution.py:16
